TPU v7x, 32 devices: a whole 2x2x4 slice. The times are simulated.
32 devices in a mesh: ctx: 16 (over z, y, core), tp: 2 (over x).
Axes of the slice: x: 2, y: 2, z: 4, core: 2. Of those that a mesh axis runs over, the one named last changes fastest.
Arguments:
- query_se: bfloat16 [3584, 8192], P('ctx', 'tp'), may hold values from -6 to 6
- key_se: bfloat16 [3584, 8192], P('ctx', 'tp'), may hold values from -6 to 6
- value_se: bfloat16 [3584, 8192], P('ctx', 'tp'), may hold values from -6 to 6
- query_mr: bfloat16 [3584, 8192], P('ctx', 'tp'), may hold values from -6 to 6
- key_mr: bfloat16 [3584, 8192], P('ctx', 'tp'), may hold values from -6 to 6
- upstream: bfloat16 [3584, 8192], P('ctx', 'tp'), may hold values from -6 to 6
- filter_se: float32 [7, 8192], P(None, 'tp'), may hold values from -2 to 2
- filter_mr: float32 [128, 8192], P(None, 'tp'), may hold values from -0.5 to 0.5
- skip_mr: float32 [8192], P('tp'), may hold values from -1 to 1
- norm_gain: float32 [8192], P('tp'), may hold values from 0.1 to 1.9
Outputs:
- grad_query_se: bfloat16 [3584, 8192], P('ctx', 'tp')
- grad_key_se: bfloat16 [3584, 8192], P('ctx', 'tp')
- grad_value_se: bfloat16 [3584, 8192], P('ctx', 'tp')
- grad_query_mr: bfloat16 [3584, 8192], P('ctx', 'tp')
- grad_key_mr: bfloat16 [3584, 8192], P('ctx', 'tp')
- grad_filter_se: float32 [7, 8192], P(None, ('tp', 'ctx'))
- grad_filter_mr: float32 [128, 8192], P(None, ('tp', 'ctx'))
- grad_skip: float32 [8192], P(('tp', 'ctx'))
- grad_gain: float32 [8192], P(('tp', 'ctx'))
All inputs are finite; a program needn't handle non-finite values.
Results may differ from a plain program's by a relative error of at most 0.0062.
Values may be sent and summed in bfloat16 or wider, within the bound.
A program may use at most 128 MiB of HBM per device.

v0:
```python
import functools
import math

import jax
import jax.numpy as jnp
import numpy as np
from jax import lax
from jax.experimental import pallas as pl
from jax.experimental.pallas import tpu as pltpu
from jax.sharding import PartitionSpec as P

EPSILON = 0.1
F32 = jnp.float32
BF16 = jnp.bfloat16
LANES = 128
MESH = pl.DeviceIdType.MESH


def transforms(rows, taps):
    length = rows + taps
    freq = 2.0 * np.pi * (np.arange(length // 2) + 0.5) / length

    def forward(start, stop):
        angle = freq[:, None] * np.arange(start, stop)[None, :]
        return np.concatenate([np.cos(angle), -np.sin(angle)], 0)

    angle = np.arange(max(rows, taps))[:, None] * freq[None, :]
    inverse = np.concatenate([np.cos(angle), -np.sin(angle)], 1) * (2.0 / length)
    mats = forward(-taps, rows), forward(0, length), inverse
    return [jnp.asarray(m, BF16) for m in mats]


def dot(a, b):
    return jnp.dot(a, b, preferred_element_type=F32)


def spectrum_of(real, imag):
    return jnp.concatenate([real.astype(BF16), imag.astype(BF16)], 0)


def up_to(value, step):
    return -(-value // step) * step


def layer_kernel(width, nctx, ntp, *refs):
    (q_h, k_h, v_h, qm_h, km_h, up_h, fse_h, fmr_h, skip_h, gain_h, fg_h, fz_h, inv_h,
     gq_o, gk_o, gv_o, gqm_o, gkm_o, corr_o, small_o,
     q, k, v, qm, km, up, fse, fmr, skip, gain, fg, fz, inv,
     ends, tail_out, tail_in, head_out, head_in,
     gfull, zfull, conv, normed, gn, hs, zs, prod, pad_g, corr, small,
     acc, scale, coef, row_out, row_in,
     in_sem, small_sem, out_sem, edge_send, edge_recv, head_send, head_recv, tail_send, tail_recv,
     row_send, row_recv) = refs
    nblk, rows, blk = q.shape
    taps_se, taps = fse.shape[1], fmr.shape[1]
    halo = tail_in.shape[0]
    half = fg.shape[0] // 2
    parts, _, group = corr.shape
    ppb = parts // nblk
    cpb = blk // LANES
    ctx, tp = lax.axis_index("ctx"), lax.axis_index("tp")
    first, last = ctx == 0, ctx == nctx - 1

    def cols_of(c):
        return pl.ds(pl.multiple_of(c * blk, blk), blk)

    def local(src, dst, sem):
        return pltpu.make_async_copy(src, dst, sem)

    def remote(src, dst, send, recv, where):
        return pltpu.make_async_remote_copy(
            src_ref=src, dst_ref=dst, send_sem=send, recv_sem=recv,
            device_id=where, device_id_type=MESH,
        )

    streams = ((up_h, up), (qm_h, qm), (k_h, k), (v_h, v), (q_h, q), (km_h, km), (fmr_h, fmr))

    def load(s, c):
        src, dst = streams[s]
        return local(src.at[:, cols_of(c)], dst.at[c], in_sem.at[s, c])

    def wide(s, c):
        src, dst = ((fse_h, fse), (skip_h, skip), (gain_h, gain))[s]
        return local(src.at[:, cols_of(c)], dst.at[c], small_sem.at[s, c])

    def whole(s):
        src, dst = ((fg_h, fg), (fz_h, fz), (inv_h, inv))[s]
        return local(src, dst, edge_send.at[2 + s])

    end_k = local(k_h.at[pl.ds(rows - halo, halo), :], ends.at[0], edge_send.at[5])
    end_v = local(v_h.at[pl.ds(rows - halo, halo), :], ends.at[1], edge_send.at[6])
    end_k.start()
    end_v.start()

    def start(*which):
        def step(c, carry):
            for s in which:
                load(s, c).start()
            return carry
        lax.fori_loop(0, nblk, step, 0)

    start(0, 1)

    def start_wide(c, carry):
        for s in range(3):
            wide(s, c).start()
        return carry

    lax.fori_loop(0, nblk, start_wide, 0)
    start(2, 3, 4)
    for s in range(3):
        whole(s).start()
    start(6)
    start(5)

    barrier = pltpu.get_barrier_semaphore()

    def greet(**where):
        pl.semaphore_signal(barrier, inc=1, device_id=where, device_id_type=MESH)

    before, after = {"ctx": ctx - 1}, {"ctx": ctx + 1}
    pl.when(ctx > 0)(lambda: greet(ctx=ctx - 1))
    pl.when(ctx < nctx - 1)(lambda: greet(ctx=ctx + 1))
    for step in range(1, ntp):
        greet(tp=lax.rem(tp + step, ntp))
    pl.semaphore_wait(
        barrier, ntp - 1 + (ctx > 0).astype(jnp.int32) + (ctx < nctx - 1).astype(jnp.int32)
    )

    tail_se = remote(tail_out, tail_in, edge_send.at[0], edge_recv.at[0], after)
    head_se = remote(head_out, head_in, edge_send.at[1], edge_recv.at[1], before)

    def head_mr(c):
        return remote(gfull.at[c, pl.ds(0, taps), :], gfull.at[c, pl.ds(rows, taps), :],
                      head_send.at[c], head_recv.at[c], before)

    def tail_mr(c):
        return remote(zfull.at[c, pl.ds(rows, taps), :], zfull.at[c, pl.ds(0, taps), :],
                      tail_send.at[c], tail_recv.at[c], after)

    end_k.wait()
    end_v.wait()
    tail_out[...] = (ends[0].astype(F32) * ends[1].astype(F32)).astype(BF16)
    pl.when(ctx < nctx - 1)(tail_se.start)

    @pl.when(first)
    def _():
        tail_in[...] = jnp.zeros_like(tail_in)
        zfull[:, :taps, :] = jnp.zeros((nblk, taps, blk), BF16)

    @pl.when(last)
    def _():
        head_in[...] = jnp.zeros_like(head_in)
        gfull[:, rows:, :] = jnp.zeros((nblk, taps, blk), BF16)

    def gate_step(c, carry):
        load(0, c).wait()
        load(1, c).wait()
        gfull[c, :rows, :] = (up[c].astype(F32) * qm[c].astype(F32)).astype(BF16)
        pl.when(ctx > 0)(lambda: head_mr(c).start())
        return carry

    lax.fori_loop(0, nblk, gate_step, 0)

    acc[...] = jnp.zeros_like(acc)
    pl.when(ctx > 0)(tail_se.wait_recv)

    def short_step(c, carry):
        for s in range(3):
            wide(s, c).wait()
            load(2 + s, c).wait()
        for i in range(cpb):
            cols = slice(i * LANES, (i + 1) * LANES)
            lane = c * cpb + i
            at = pl.ds(pl.multiple_of(lane * LANES, LANES), LANES)
            prod[lane, :halo, :] = tail_in[:, at].astype(F32)
            product = k[c, :, cols].astype(F32) * v[c, :, cols].astype(F32)
            prod[lane, halo:, :] = product.astype(BF16).astype(F32)
            out = fse[c, 0:1, cols] * prod[lane, pl.ds(halo, rows), :]
            for j in range(1, taps_se):
                out = out + fse[c, j : j + 1, cols] * prod[lane, pl.ds(halo - j, rows), :]
            conv[c, :, cols] = out
            mixed = q[c, :, cols].astype(F32) * out
            acc[:rows, :] += mixed * mixed
        return carry

    lax.fori_loop(0, nblk, short_step, 0)

    def row_copy(which, step):
        return remote(row_out.at[which], row_in.at[which, step - 1],
                      row_send.at[which, step - 1], row_recv.at[which, step - 1],
                      {"tp": lax.rem(tp + step, ntp)})

    def send_rows(which):
        total = jnp.sum(jnp.transpose(acc[...]), axis=0, keepdims=True)
        row_out[which] = jnp.broadcast_to(total, row_out.shape[1:])
        for step in range(1, ntp):
            row_copy(which, step).start()

    def sum_rows(which):
        total = row_out[which]
        for step in range(1, ntp):
            row_copy(which, step).wait_recv()
            total = total + row_in[which, step - 1]
        return total[0:1, :]

    def as_column(line):
        return jnp.transpose(jnp.broadcast_to(line, (LANES, line.shape[1])))[:rows, :]

    send_rows(0)

    for s in range(3):
        whole(s).wait()

    def filter_step(c, carry):
        load(6, c).wait()
        spec = dot(fz[:, taps : 2 * taps], fmr[c].astype(BF16))
        hs[c, :half, :] = spec[:half] + skip[c]
        hs[c, half:, :] = spec[half:]
        return carry

    lax.fori_loop(0, nblk, filter_step, 0)

    scale[...] = as_column(lax.rsqrt(sum_rows(0) * (1.0 / width) + EPSILON))

    def product_step(c, carry):
        load(5, c).wait()
        for i in range(cpb):
            cols = slice(i * LANES, (i + 1) * LANES)
            mixed = q[c, :, cols].astype(F32) * conv[c, :, cols]
            value = mixed * scale[...] * gain[c, :, cols]
            normed[c, :, cols] = value
            zfull[c, taps:, cols] = (km[c, :, cols].astype(F32) * value).astype(BF16)
        pl.when(ctx < nctx - 1)(lambda: tail_mr(c).start())
        return carry

    lax.fori_loop(0, nblk, product_step, 0)

    acc[...] = jnp.zeros_like(acc)

    def adjoint_step(c, carry):
        pl.when(ctx < nctx - 1)(lambda: head_mr(c).wait_recv())
        gs = dot(fg[...], gfull[c])
        gr, gi = gs[:half], gs[half:]
        hr, hi = hs[c, :half, :], hs[c, half:, :]
        gp = dot(inv[:rows, :], spectrum_of(gr * hr + gi * hi, gi * hr - gr * hi))
        for i in range(cpb):
            cols = slice(i * LANES, (i + 1) * LANES)
            back, value = gp[:, cols], normed[c, :, cols]
            grad = back * km[c, :, cols].astype(F32)
            qm[c, :, cols] = (back * value).astype(BF16)
            gn[c, :, cols] = grad
            acc[:rows, :] += grad * value
        local(qm.at[c], gkm_o.at[:, cols_of(c)], out_sem.at[0, c]).start()
        spec = dot(fz[:, taps:], zfull[c, taps:, :])
        zs[c] = spec
        zr, zi = spec[:half], spec[half:]
        part = dot(inv[:taps, :], spectrum_of(gr * zr + gi * zi, gi * zr - gr * zi))
        for p in range(ppb):
            corr[c * ppb + p] = part[:, p * group : (p + 1) * group]
        return carry

    lax.fori_loop(0, nblk, adjoint_step, 0)
    corr_copy = local(corr, corr_o, out_sem.at[5, 0])
    corr_copy.start()

    send_rows(1)

    def medium_step(c, carry):
        pl.when(ctx > 0)(lambda: tail_mr(c).wait_recv())
        spec = zs[c] + dot(fz[:, :taps], zfull[c, :taps, :])
        zr, zi = spec[:half], spec[half:]
        hr, hi = hs[c, :half, :], hs[c, half:, :]
        out = dot(inv[:rows, :], spectrum_of(zr * hr - zi * hi, zr * hi + zi * hr))
        up[c] = (up[c].astype(F32) * out).astype(BF16)
        local(up.at[c], gqm_o.at[:, cols_of(c)], out_sem.at[1, c]).start()
        return carry

    lax.fori_loop(0, nblk // 2, medium_step, 0)

    weight = as_column(sum_rows(1))
    coef[...] = weight * (scale[...] * scale[...]) * (1.0 / width)

    def grad_mixed(c, cols, top):
        at = slice(0, top)
        back = gn[c, at, cols] * scale[at, :]
        quer = q[c, at, cols].astype(F32)
        mixed = quer * conv[c, at, cols]
        return back, quer, mixed, gain[c, :, cols] * back - mixed * coef[at, :]

    def edge_step(c, carry):
        for i in range(cpb):
            cols = slice(i * LANES, (i + 1) * LANES)
            at = pl.ds(pl.multiple_of(c * blk + i * LANES, LANES), LANES)
            _, quer, _, gm = grad_mixed(c, cols, halo)
            head_out[:, at] = (gm * quer).astype(BF16)
        return carry

    lax.fori_loop(0, nblk, edge_step, 0)
    pl.when(ctx > 0)(head_se.start)

    lax.fori_loop(nblk // 2, nblk, medium_step, 0)

    pl.when(ctx < nctx - 1)(head_se.wait_recv)

    def back_step(c, carry):
        for i in range(cpb):
            cols = slice(i * LANES, (i + 1) * LANES)
            lane = c * cpb + i
            at = pl.ds(pl.multiple_of(lane * LANES, LANES), LANES)
            back, quer, mixed, gm = grad_mixed(c, cols, rows)
            gc = (gm * quer).astype(BF16).astype(F32)
            pad_g[i, :rows, :] = gc
            pad_g[i, rows:, :] = head_in[:, at].astype(F32)
            part, inner = i * LANES // group, i * LANES % group
            place = slice(inner, inner + LANES)
            small[c * ppb + part, taps_se : taps_se + 1, place] = jnp.sum(
                back * mixed, axis=0, keepdims=True
            )
            q[c, :, cols] = (gm * conv[c, :, cols]).astype(BF16)
            gp = fse[c, 0:1, cols] * gc
            for j in range(taps_se):
                if j:
                    gp = gp + fse[c, j : j + 1, cols] * pad_g[i, pl.ds(j, rows), :]
                small[c * ppb + part, j : j + 1, place] = jnp.sum(
                    gc * prod[lane, pl.ds(halo - j, rows), :], axis=0, keepdims=True
                )
            key = k[c, :, cols].astype(F32)
            k[c, :, cols] = (gp * v[c, :, cols].astype(F32)).astype(BF16)
            v[c, :, cols] = (gp * key).astype(BF16)
        for s, (src, dst) in enumerate(((q, gq_o), (k, gk_o), (v, gv_o))):
            local(src.at[c], dst.at[:, cols_of(c)], out_sem.at[2 + s, c]).start()
        return carry

    lax.fori_loop(0, nblk, back_step, 0)
    small_copy = local(small, small_o, out_sem.at[5, 1])
    small_copy.start()

    def finish(c, carry):
        pairs = ((qm, gkm_o), (up, gqm_o), (q, gq_o), (k, gk_o), (v, gv_o))
        for s, (src, dst) in enumerate(pairs):
            local(src.at[c], dst.at[:, cols_of(c)], out_sem.at[s, c]).wait()
        pl.when(ctx > 0)(lambda: head_mr(c).wait_send())
        pl.when(ctx < nctx - 1)(lambda: tail_mr(c).wait_send())
        return carry

    lax.fori_loop(0, nblk, finish, 0)
    corr_copy.wait()
    small_copy.wait()
    pl.when(ctx < nctx - 1)(tail_se.wait_send)
    pl.when(ctx > 0)(head_se.wait_send)
    for which in range(2):
        for step in range(1, ntp):
            row_copy(which, step).wait_send()


def split_parts(parts, share):
    count, height, group = parts.shape
    if group == share:
        return parts
    parts = parts.reshape(count, height, group // share, share)
    return parts.transpose(0, 2, 1, 3).reshape(-1, height, share)


def scatter_sum(parts, axis):
    size = lax.axis_size(axis)
    me = lax.axis_index(axis)
    bit = 1
    while bit < size:
        rest = parts.reshape((parts.shape[0] // 2, 2) + parts.shape[1:])
        mine = lax.rem(me // bit, 2)
        away = lax.dynamic_index_in_dim(rest, 1 - mine, 1, keepdims=False).astype(BF16)
        keep = lax.dynamic_index_in_dim(rest, mine, 1, keepdims=False)
        with jax.named_scope(f"halve_{bit}"):
            got = lax.ppermute(away, axis, [(i, i ^ bit) for i in range(size)])
        parts = keep + got.astype(F32)
        bit *= 2
    return parts[0]


def local(
    query_se, key_se, value_se, query_mr, key_mr, upstream, filter_se, filter_mr, skip_mr, norm_gain
):
    rows, chans = query_se.shape
    taps_se, taps = filter_se.shape[0], filter_mr.shape[0]
    ctx, ntp = lax.axis_size("ctx"), lax.axis_size("tp")
    width = chans * ntp
    tokens = rows * ctx
    share = chans // ctx
    group = up_to(share, LANES)
    halo = up_to(taps_se - 1, 16)
    blk = max(group, min(512, chans))
    nblk = chans // blk
    fz, fg, inv = transforms(rows, taps)
    length = rows + taps
    tall = up_to(rows, LANES)
    nlane = chans // LANES

    def out(shape, kind):
        return jax.ShapeDtypeStruct(shape, kind)

    ins = (query_se, key_se, value_se, query_mr, key_mr, upstream, filter_se, filter_mr,
           skip_mr[None], norm_gain[None], fg, fz, inv)
    outs = [out((rows, chans), BF16)] * 5 + [
        out((chans // group, taps, group), F32), out((chans // group, taps_se + 1, group), F32)
    ]
    V, D = pltpu.VMEM, pltpu.SemaphoreType.DMA
    stream = V((nblk, rows, blk), BF16)
    scratch = [stream] * 6 + [
        V((nblk, taps_se, blk), F32), V((nblk, taps, blk), F32), V((nblk, 1, blk), F32),
        V((nblk, 1, blk), F32), V(fg.shape, BF16), V(fz.shape, BF16), V(inv.shape, BF16),
        V((2, halo, chans), BF16), V((halo, chans), BF16), V((halo, chans), BF16),
        V((halo, chans), BF16), V((halo, chans), BF16),
        V((nblk, length, blk), BF16), V((nblk, length, blk), BF16),
        V((nblk, rows, blk), F32), V((nblk, rows, blk), F32), V((nblk, rows, blk), F32),
        V((nblk, length, blk), F32), V((nblk, length, blk), F32),
        V((nlane, halo + rows, LANES), F32), V((blk // LANES, halo + rows, LANES), F32),
        V(outs[5].shape, F32), V(outs[6].shape, F32),
        V((tall, LANES), F32), V((rows, LANES), F32), V((rows, LANES), F32),
        V((2, 8, tall), F32), V((2, max(ntp - 1, 1), 8, tall), F32),
        D((7, nblk)), D((3, nblk)), D((6, max(nblk, 2))), D((7,)), D((2,)),
        D((nblk,)), D((nblk,)), D((nblk,)), D((nblk,)),
        D((2, max(ntp - 1, 1))), D((2, max(ntp - 1, 1))),
    ]
    anywhere = pl.BlockSpec(memory_space=pl.ANY)
    with jax.named_scope("layer"):
        (grad_query_se, grad_key_se, grad_value_se, grad_query_mr, grad_key_mr, corr,
         small) = pl.pallas_call(
            functools.partial(layer_kernel, width, ctx, ntp),
            name="layer",
            in_specs=[anywhere] * len(ins),
            out_specs=[anywhere] * len(outs),
            out_shape=outs,
            scratch_shapes=scratch,
            compiler_params=pltpu.CompilerParams(
                collective_id=0, has_side_effects=True, vmem_limit_bytes=62 * 2**20
            ),
        )(*ins)
    corr, small = split_parts(corr, share), split_parts(small, share)
    small = lax.all_to_all(small, "ctx", 0, 0, tiled=True)
    factor = 1.0 / math.sqrt(tokens)
    total_mr = scatter_sum(corr, "ctx") * factor
    total = jnp.sum(small, axis=0) * factor
    return (
        grad_query_se,
        grad_key_se,
        grad_value_se,
        grad_query_mr,
        grad_key_mr,
        total[:taps_se],
        total_mr,
        total_mr[0],
        total[taps_se],
    )


def solution(mesh):
    streams = (P("ctx", "tp"),)
    in_specs = streams * 6 + (P(None, "tp"), P(None, "tp"), P("tp"), P("tp"))
    both = ("tp", "ctx")
    out_specs = streams * 5 + (P(None, both), P(None, both), P(both), P(both))
    return jax.shard_map(local, mesh=mesh, in_specs=in_specs, out_specs=out_specs, check_vma=False)
```

profile of v0, /device:TPU:0, one launch (start us, length us, event | category | flops | bytes accessed | tf_op | source)
XLA Modules:
  0.0 89.0 jit_solution(445894309550357270)
XLA Ops:
  0.7 37.8 %layer.1 = (bf16[224,4096]{1,0:T(8,128)(2,1)}, bf16[224,4096]{1,0:T(8,128)(2,1)}, bf16[224,4096]{1,0:T(8,128)(2,1)}, bf16[224,4096]{1,0:T(8,128)(2,1)}, bf16[224...) custom-call(bf16[224,4096]{1,0:T(8,128)(2,1)} %refs_0_.1, bf16[224,4096]{1,0:T(8,128)(2,1)} %refs_1_.1, ...), custom_call_target="tpu_custom_call" | custom-call | tf_op jit(solution)/shard_map/layer/layer/pallas_call | solution.py:428
  38.4 1.3 %fusion = bf16[8,128,256]{2,1,0:T(8,128)(2,1)S(1)} fusion(f32[8,2,128,256]{3,2,1,0:T(8,128)} %bitcast.29, s32[]{:T(128)S(6)} %select_n.41), kind=kLoop, calls=%fused_computation.2 | loop fusion | bytes 1048580 | tf_op jit(solution)/shard_map/convert_element_type | solution.py:372
  39.7 15.6 %collective-permute-start = (bf16[8,128,256]{2,1,0:T(8,128)(2,1)S(1)}, bf16[8,128,256]{2,1,0:T(8,128)(2,1)S(1)}, u32[]{:S(2)}, u32[]{:S(2)}) collective-permute-start(bf16[8,128,256]{2,1,0:T(8,128)(2,1)S(1)} %fusion), channel_id=1, source_target_pairs={{0,2},{2,0},{4,6},{6,4},{8,10},{10,8},{12,14},{14,12},{16,18},{18,... | collective-permute-start | bytes 1572872 | tf_op jit(solution)/shard_map/halve_1/ppermute | solution.py:375
  55.3 1.5 %collective-permute-done = bf16[8,128,256]{2,1,0:T(8,128)(2,1)S(1)} collective-permute-done((bf16[8,128,256]{2,1,0:T(8,128)(2,1)S(1)}, bf16[8,128,256]{2,1,0:T(8,128)(2,1)S(1)}, u32[]{:S(2)}, u32[]{:S(2)}) %collective-permute-start) | collective-permute-done | bytes 524320 | tf_op jit(solution)/shard_map/halve_1/ppermute | solution.py:375
  56.9 1.3 %bitcast_add_fusion = f32[8,128,256]{2,1,0:T(8,128)S(1)} fusion(bf16[8,128,256]{2,1,0:T(8,128)(2,1)S(1)} %collective-permute-done, f32[8,2,128,256]{3,2,1,0:T(8,128)} %bitcast.30, s32[]{:T(128)S(6)} %select_n.40), kind=kLoop, calls=%fused_computation.1 | loop fusion | flops 524288 | bytes 2621444 | tf_op jit(solution)/shard_map/add | solution.py:376
  58.2 0.0 copy-start.4
  58.3 0.1 collective-permute-start.1
  58.3 5.4 %all-to-all-start = ((f32[16,8,256]{2,1,0:T(8,128)}), f32[16,8,256]{2,1,0:T(8,128)S(1)}, u32[]{:S(2)}, u32[]{:S(2)}) async-start(f32[16,8,256]{2,1,0:T(8,128)} %get-tuple-element.21), calls=%async_computation | async-start | bytes 262144 | tf_op jit(solution)/shard_map/all_to_all | solution.py:440
  63.8 3.3 %collective-permute-done.1 = bf16[4,128,256]{2,1,0:T(8,128)(2,1)} collective-permute-done((bf16[4,128,256]{2,1,0:T(8,128)(2,1)S(1)}, bf16[4,128,256]{2,1,0:T(8,128)(2,1)}, u32[]{:S(2)}, u32[]{:S(2)}) %collective-permute-start.1) | collective-permute-done | bytes 262176 | tf_op jit(solution)/shard_map/halve_2/ppermute | solution.py:375
  67.1 1.0 %bitcast_add_fusion.1 = f32[4,128,256]{2,1,0:T(8,128)S(1)} fusion(bf16[4,128,256]{2,1,0:T(8,128)(2,1)} %collective-permute-done.1, f32[4,2,128,256]{3,2,1,0:T(8,128)S(1)} %bitcast.26, s32[]{:T(128)S(6)} %select_n.43), kind=kLoop, calls=%fused_computation.3 | loop fusion | flops 262144 | bytes 1310724 | tf_op jit(solution)/shard_map/add | solution.py:376
  68.1 1.8 %collective-permute-start.2 = (bf16[2,128,256]{2,1,0:T(8,128)(2,1)S(1)}, bf16[2,128,256]{2,1,0:T(8,128)(2,1)S(1)}, u32[]{:S(2)}, u32[]{:S(2)}) collective-permute-start(bf16[2,128,256]{2,1,0:T(8,128)(2,1)S(1)} %fusion.2), channel_id=1, source_target_pairs={{0,8},{2,10},{4,12},{6,14},{8,0},{10,2},{12,4},{14,6},{16,24},{18,... | collective-permute-start | bytes 393224 | tf_op jit(solution)/shard_map/halve_4/ppermute | solution.py:375
  69.9 1.8 %all-to-all-done = f32[16,8,256]{2,1,0:T(8,128)S(1)} async-done(((f32[16,8,256]{2,1,0:T(8,128)}), f32[16,8,256]{2,1,0:T(8,128)S(1)}, u32[]{:S(2)}, u32[]{:S(2)}) %all-to-all-start) | async-done | bytes 131104 | tf_op jit(solution)/shard_map/all_to_all | solution.py:440
  71.7 1.5 %collective-permute-done.2 = bf16[2,128,256]{2,1,0:T(8,128)(2,1)S(1)} collective-permute-done((bf16[2,128,256]{2,1,0:T(8,128)(2,1)S(1)}, bf16[2,128,256]{2,1,0:T(8,128)(2,1)S(1)}, u32[]{:S(2)}, u32[]{:S(2)}) %collective-permute-start.2) | collective-permute-done | bytes 131104 | tf_op jit(solution)/shard_map/halve_4/ppermute | solution.py:375
  73.3 2.8 %collective-permute-start.3 = (bf16[1,128,256]{2,1,0:T(8,128)(2,1)S(1)}, bf16[1,128,256]{2,1,0:T(8,128)(2,1)S(1)}, u32[]{:S(2)}, u32[]{:S(2)}) collective-permute-start(bf16[1,128,256]{2,1,0:T(8,128)(2,1)S(1)} %dynamic-slice_convert_fusion.2), channel_id=1, source_target_pairs={{0,16},{2,18},{4,20},{6,22},{8,24},{10,26},{12,28},{14,30},{16,0},... | collective-permute-start | bytes 196616 | tf_op jit(solution)/shard_map/halve_8/ppermute | solution.py:375
  76.1 0.0 copy-start.6
  76.1 0.6 slice.15
  76.6 1.9 %collective-permute-done.3 = bf16[1,128,256]{2,1,0:T(8,128)(2,1)S(1)} collective-permute-done((bf16[1,128,256]{2,1,0:T(8,128)(2,1)S(1)}, bf16[1,128,256]{2,1,0:T(8,128)(2,1)S(1)}, u32[]{:S(2)}, u32[]{:S(2)}) %collective-permute-start.3) | collective-permute-done | bytes 65568 | tf_op jit(solution)/shard_map/halve_8/ppermute | solution.py:375
  78.5 0.0 copy-start.5
  78.5 0.6 slice.14
  79.1 0.0 copy-done.4
  79.1 0.0 copy-start.3
  79.1 1.2 %copy.29 = bf16[224,4096]{1,0:T(8,128)(2,1)} copy(bf16[224,4096]{1,0:T(8,128)(2,1)S(1)} %copy-done.4) | data formatting | bytes 3670016
  80.4 0.0 copy-done.6
  80.4 0.0 copy-done.5
  80.4 0.9 %copy-done.3 = bf16[224,4096]{1,0:T(8,128)(2,1)S(1)} copy-done((bf16[224,4096]{1,0:T(8,128)(2,1)S(1)}, bf16[224,4096]{1,0:T(8,128)(2,1)}, u32[]{:S(2)}) %copy-start.3) | copy-done | bytes 1835032
  81.3 0.0 copy-start.2
  81.3 1.2 %copy.30 = bf16[224,4096]{1,0:T(8,128)(2,1)} copy(bf16[224,4096]{1,0:T(8,128)(2,1)S(1)} %copy-done.3) | data formatting | bytes 3670016
  82.5 0.9 %copy-done.2 = bf16[224,4096]{1,0:T(8,128)(2,1)S(1)} copy-done((bf16[224,4096]{1,0:T(8,128)(2,1)S(1)}, bf16[224,4096]{1,0:T(8,128)(2,1)}, u32[]{:S(2)}) %copy-start.2) | copy-done | bytes 1835032
  83.5 0.0 copy-start.1
  83.5 1.2 %copy.31 = bf16[224,4096]{1,0:T(8,128)(2,1)} copy(bf16[224,4096]{1,0:T(8,128)(2,1)S(1)} %copy-done.2) | data formatting | bytes 3670016
  84.7 0.9 %copy-done.1 = bf16[224,4096]{1,0:T(8,128)(2,1)S(1)} copy-done((bf16[224,4096]{1,0:T(8,128)(2,1)S(1)}, bf16[224,4096]{1,0:T(8,128)(2,1)}, u32[]{:S(2)}) %copy-start.1) | copy-done | bytes 1835032
  85.6 0.0 copy-start
  85.6 1.2 %copy.32 = bf16[224,4096]{1,0:T(8,128)(2,1)} copy(bf16[224,4096]{1,0:T(8,128)(2,1)S(1)} %copy-done.1) | data formatting | bytes 3670016
  86.9 0.9 %copy-done = bf16[224,4096]{1,0:T(8,128)(2,1)S(1)} copy-done((bf16[224,4096]{1,0:T(8,128)(2,1)S(1)}, bf16[224,4096]{1,0:T(8,128)(2,1)}, u32[]{:S(2)}) %copy-start) | copy-done | bytes 1835032
  87.8 1.2 %copy.33 = bf16[224,4096]{1,0:T(8,128)(2,1)} copy(bf16[224,4096]{1,0:T(8,128)(2,1)S(1)} %copy-done) | data formatting | bytes 3670016
  (7 shorter events, 0.1 us)
Async XLA Ops:
  39.7 17.1 %collective-permute-start = (bf16[8,128,256]{2,1,0:T(8,128)(2,1)S(1)}, bf16[8,128,256]{2,1,0:T(8,128)(2,1)S(1)}, u32[]{:S(2)}, u32[]{:S(2)}) collective-permute-start(bf16[8,128,256]{2,1,0:T(8,128)(2,1)S(1)} %fusion), channel_id=1, source_target_pairs={{0,2},{2,0},{4,6},{6,4},{8,10},{10,8},{12,14},{14,12},{16,18},{18,... | collective-permute-start | bytes 1572872 | tf_op jit(solution)/shard_map/halve_1/ppermute | solution.py:375
  58.2 20.9 %copy-start.4 = (bf16[224,4096]{1,0:T(8,128)(2,1)S(1)}, bf16[224,4096]{1,0:T(8,128)(2,1)}, u32[]{:S(2)}) copy-start(bf16[224,4096]{1,0:T(8,128)(2,1)} %get-tuple-element.32) | copy-start | bytes 5505028
  58.3 8.8 %collective-permute-start.1 = (bf16[4,128,256]{2,1,0:T(8,128)(2,1)S(1)}, bf16[4,128,256]{2,1,0:T(8,128)(2,1)}, u32[]{:S(2)}, u32[]{:S(2)}) collective-permute-start(bf16[4,128,256]{2,1,0:T(8,128)(2,1)S(1)} %fusion.1), channel_id=1, source_target_pairs={{0,4},{2,6},{4,0},{6,2},{8,12},{10,14},{12,8},{14,10},{16,20},{18,... | collective-permute-start | bytes 786440 | tf_op jit(solution)/shard_map/halve_2/ppermute | solution.py:375
  58.3 13.3 %all-to-all-start = ((f32[16,8,256]{2,1,0:T(8,128)}), f32[16,8,256]{2,1,0:T(8,128)S(1)}, u32[]{:S(2)}, u32[]{:S(2)}) async-start(f32[16,8,256]{2,1,0:T(8,128)} %get-tuple-element.21), calls=%async_computation | async-start | bytes 262144 | tf_op jit(solution)/shard_map/all_to_all | solution.py:440
  68.1 5.1 %collective-permute-start.2 = (bf16[2,128,256]{2,1,0:T(8,128)(2,1)S(1)}, bf16[2,128,256]{2,1,0:T(8,128)(2,1)S(1)}, u32[]{:S(2)}, u32[]{:S(2)}) collective-permute-start(bf16[2,128,256]{2,1,0:T(8,128)(2,1)S(1)} %fusion.2), channel_id=1, source_target_pairs={{0,8},{2,10},{4,12},{6,14},{8,0},{10,2},{12,4},{14,6},{16,24},{18,... | collective-permute-start | bytes 393224 | tf_op jit(solution)/shard_map/halve_4/ppermute | solution.py:375
  73.3 5.2 %collective-permute-start.3 = (bf16[1,128,256]{2,1,0:T(8,128)(2,1)S(1)}, bf16[1,128,256]{2,1,0:T(8,128)(2,1)S(1)}, u32[]{:S(2)}, u32[]{:S(2)}) collective-permute-start(bf16[1,128,256]{2,1,0:T(8,128)(2,1)S(1)} %dynamic-slice_convert_fusion.2), channel_id=1, source_target_pairs={{0,16},{2,18},{4,20},{6,22},{8,24},{10,26},{12,28},{14,30},{16,0},... | collective-permute-start | bytes 196616 | tf_op jit(solution)/shard_map/halve_8/ppermute | solution.py:375
  76.1 4.3 %copy-start.6 = (f32[8,256]{1,0:T(8,128)}, f32[8,256]{1,0:T(8,128)S(1)}, u32[]{:S(2)}) copy-start(f32[8,256]{1,0:T(8,128)S(1)} %broadcast_multiply_fusion) | copy-start | bytes 24580
  78.5 1.8 %copy-start.5 = (f32[1,128,256]{2,1,0:T(8,128)}, f32[1,128,256]{2,1,0:T(8,128)S(1)}, u32[]{:S(2)}) copy-start(f32[1,128,256]{2,1,0:T(8,128)S(1)} %add_multiply_fusion) | copy-start | bytes 393220
  79.1 2.2 %copy-start.3 = (bf16[224,4096]{1,0:T(8,128)(2,1)S(1)}, bf16[224,4096]{1,0:T(8,128)(2,1)}, u32[]{:S(2)}) copy-start(bf16[224,4096]{1,0:T(8,128)(2,1)} %get-tuple-element.33) | copy-start | bytes 5505028
  81.3 2.2 %copy-start.2 = (bf16[224,4096]{1,0:T(8,128)(2,1)S(1)}, bf16[224,4096]{1,0:T(8,128)(2,1)}, u32[]{:S(2)}) copy-start(bf16[224,4096]{1,0:T(8,128)(2,1)} %get-tuple-element.34) | copy-start | bytes 5505028
  83.5 2.2 %copy-start.1 = (bf16[224,4096]{1,0:T(8,128)(2,1)S(1)}, bf16[224,4096]{1,0:T(8,128)(2,1)}, u32[]{:S(2)}) copy-start(bf16[224,4096]{1,0:T(8,128)(2,1)} %get-tuple-element.35) | copy-start | bytes 5505028
  85.6 2.2 %copy-start = (bf16[224,4096]{1,0:T(8,128)(2,1)S(1)}, bf16[224,4096]{1,0:T(8,128)(2,1)}, u32[]{:S(2)}) copy-start(bf16[224,4096]{1,0:T(8,128)(2,1)} %get-tuple-element.36) | copy-start | bytes 5505028
where the time goes:
time: 89.5 us; the launch traced here: 89 us
  Pallas kernels  37.8 us (42%)
  starting transfers between devices  25.6 us (29%)
  local copies, waits for them, and re-layouts  12.4 us (14%)
  waiting for transfers between devices  10 us (11%)
  other arithmetic  2.41 us (3%)
    pallas_call x1, Pallas kernels, local(): pl.pallas_call(functools.partial(layer_kernel, width, ctx, ntp), name='la...  37.8 us
    ppermute x4, starting transfers between devices, scatter_sum(): got = lax.ppermute(away, axis, [(i, i ^ bit) for i in range(size)])  20.2 us
    unnamed x19, local copies, waits for them, and re-layouts  9.88 us
    ppermute x4, waiting for transfers between devices, scatter_sum(): got = lax.ppermute(away, axis, [(i, i ^ bit) for i in range(size)])  8.18 us
    all_to_all x1, starting transfers between devices, local(): small = lax.all_to_all(small, 'ctx', 0, 0, tiled=True)  5.42 us
    add x3, other arithmetic, scatter_sum(): parts = keep + got.astype(F32)  2.37 us
    all_to_all x1, waiting for transfers between devices, local(): small = lax.all_to_all(small, 'ctx', 0, 0, tiled=True)  1.82 us
  transfers between devices with their start and end apart: 5, of which 5 were waited for; matrix products, arithmetic and copies ran while one was open for 2% of the time, Pallas kernels for 0%

commit v1 on v0

v1 whole, which is shorter than its diff:
```python
import functools
import math

import jax
import jax.numpy as jnp
import numpy as np
from jax import lax
from jax.experimental import pallas as pl
from jax.experimental.pallas import tpu as pltpu
from jax.sharding import PartitionSpec as P

EPSILON = 0.1
F32 = jnp.float32
BF16 = jnp.bfloat16
LANES = 128
MESH = pl.DeviceIdType.MESH


def transforms(rows, taps):
    length = rows + taps
    freq = 2.0 * np.pi * (np.arange(length // 2) + 0.5) / length

    def forward(start, stop):
        angle = freq[:, None] * np.arange(start, stop)[None, :]
        return np.concatenate([np.cos(angle), -np.sin(angle)], 0)

    angle = np.arange(max(rows, taps))[:, None] * freq[None, :]
    inverse = np.concatenate([np.cos(angle), -np.sin(angle)], 1) * (2.0 / length)
    mats = forward(-taps, rows), forward(0, length), inverse
    return [jnp.asarray(m, BF16) for m in mats]


def dot(a, b):
    return jnp.dot(a, b, preferred_element_type=F32)


def spectrum_of(real, imag):
    return jnp.concatenate([real.astype(BF16), imag.astype(BF16)], 0)


def up_to(value, step):
    return -(-value // step) * step


def halving_bits(size, ratio):
    bits = []
    bit = ratio
    while bit < size:
        bits.append(bit)
        bit *= 2
    return bits[:1] + bits[2:] + bits[1:2]


def runs(count):
    return 2 if count % 2 == 0 else 1


def layer_kernel(width, tokens, nctx, ntp, ratio, *refs):
    (q_h, k_h, v_h, qm_h, km_h, up_h, fse_h, fmr_h, skip_h, gain_h, fg_h, fz_h, inv_h,
     q, k, v, qm, up, total_o, small_o,
     km, fse, fmr, skip, gain, fg, fz, inv, ends, tail_out, tail_in, head_out, head_in,
     gfull, zfull, conv, normed, hs, zs, prod, pad_g, corr, small, away, got, small_in,
     acc, scale, coef, row_out, row_in,
     in_sem, small_sem, edge_sem, edge_send, edge_recv, head_send, head_recv, tail_send, tail_recv,
     row_send, row_recv, halve_send, halve_recv, swap_send, swap_recv) = refs
    nblk, rows, blk = q.shape
    taps_se, taps = fse.shape[1], fmr.shape[1]
    halo = tail_in.shape[0]
    half = fg.shape[0] // 2
    parts, _, group = corr.shape
    ppb = parts // nblk
    cpb = blk // LANES
    ctx, tp = lax.axis_index("ctx"), lax.axis_index("tp")
    first, last = ctx == 0, ctx == nctx - 1
    bits = halving_bits(nctx, ratio)
    factor = 1.0 / math.sqrt(tokens)

    def cols_of(c):
        return pl.ds(pl.multiple_of(c * blk, blk), blk)

    def each(count, body, start=0):
        def step(c, carry):
            body(c)
            return carry
        lax.fori_loop(start, start + count, step, 0)

    def several(start, stop, body):
        n = runs(stop - start)
        each((stop - start) // n, lambda p: body([start + p * n + u for u in range(n)]))

    def remote(src, dst, send, recv, where):
        return pltpu.make_async_remote_copy(
            src_ref=src, dst_ref=dst, send_sem=send, recv_sem=recv,
            device_id=where, device_id_type=MESH,
        )

    streams = ((up_h, up), (qm_h, qm), (k_h, k), (v_h, v), (q_h, q), (km_h, km), (fmr_h, fmr))

    def load(s, c):
        src, dst = streams[s]
        return pltpu.make_async_copy(src.at[:, cols_of(c)], dst.at[c], in_sem.at[s, c])

    def wide(s, c):
        src, dst = ((fse_h, fse), (skip_h, skip), (gain_h, gain))[s]
        return pltpu.make_async_copy(src.at[:, cols_of(c)], dst.at[c], small_sem.at[s, c])

    def single(s):
        bottom = pl.ds(rows - halo, halo)
        src, dst = ((k_h.at[bottom, :], ends.at[0]), (v_h.at[bottom, :], ends.at[1]),
                    (fg_h, fg), (fz_h, fz), (inv_h, inv))[s]
        return pltpu.make_async_copy(src, dst, edge_sem.at[s])

    barrier = pltpu.get_barrier_semaphore()
    for step in range(1, nctx):
        pl.semaphore_signal(barrier, inc=1, device_id={"ctx": lax.rem(ctx + step, nctx)},
                            device_id_type=MESH)
    for step in range(1, ntp):
        pl.semaphore_signal(barrier, inc=1, device_id={"tp": lax.rem(tp + step, ntp)},
                            device_id_type=MESH)

    def start_group(*which):
        def body(c):
            for s in which:
                load(s, c).start()
        each(nblk, body)

    def start_wide(c):
        for s in range(3):
            wide(s, c).start()

    single(0).start()
    single(1).start()
    start_group(0, 1)
    single(3).start()
    each(nblk, start_wide)
    start_group(6)
    start_group(2, 3, 4)
    single(2).start()
    single(4).start()
    start_group(5)

    @pl.when(first)
    def _():
        tail_in[...] = jnp.zeros_like(tail_in)
        zfull[:, :taps, :] = jnp.zeros((nblk, taps, blk), BF16)

    @pl.when(last)
    def _():
        head_in[...] = jnp.zeros_like(head_in)
        gfull[:, rows:, :] = jnp.zeros((nblk, taps, blk), BF16)

    before, after = {"ctx": ctx - 1}, {"ctx": ctx + 1}
    tail_se = remote(tail_out, tail_in, edge_send.at[0], edge_recv.at[0], after)
    head_se = remote(head_out, head_in, edge_send.at[1], edge_recv.at[1], before)

    def head_mr(c):
        return remote(gfull.at[c, pl.ds(0, taps), :], gfull.at[c, pl.ds(rows, taps), :],
                      head_send.at[c], head_recv.at[c], before)

    def tail_mr(c):
        return remote(zfull.at[c, pl.ds(rows, taps), :], zfull.at[c, pl.ds(0, taps), :],
                      tail_send.at[c], tail_recv.at[c], after)

    single(0).wait()
    single(1).wait()
    tail_out[...] = (ends[0].astype(F32) * ends[1].astype(F32)).astype(BF16)

    def gate_step(c):
        load(0, c).wait()
        load(1, c).wait()
        gfull[c, :rows, :] = (up[c].astype(F32) * qm[c].astype(F32)).astype(BF16)

    with jax.named_scope("p_gate"):
        each(nblk, gate_step)
    with jax.named_scope("p_bar"):
        pl.semaphore_wait(barrier, nctx + ntp - 2)
    pl.when(ctx < nctx - 1)(tail_se.start)
    single(3).wait()

    def filter_step(cs):
        for c in cs:
            load(6, c).wait()
            wide(1, c).wait()
        found = [dot(fz[:, taps : 2 * taps], fmr[c].astype(BF16)) for c in cs]
        for c, value in zip(cs, found):
            hs[c, :half, :] = value[:half] + skip[c]
            hs[c, half:, :] = value[half:]

    with jax.named_scope("p_filt1"):
        several(0, nblk // 2, filter_step)

    @pl.when(ctx > 0)
    def _():
        each(nblk, lambda c: head_mr(c).start())

    acc[...] = jnp.zeros_like(acc)
    with jax.named_scope("p_tailse"):
        pl.when(ctx > 0)(tail_se.wait_recv)

    def short_step(c):
        wide(0, c).wait()
        wide(2, c).wait()
        for s in range(3):
            load(2 + s, c).wait()
        for i in range(cpb):
            cols = slice(i * LANES, (i + 1) * LANES)
            lane = c * cpb + i
            at = pl.ds(pl.multiple_of(lane * LANES, LANES), LANES)
            prod[lane, :halo, :] = tail_in[:, at].astype(F32)
            product = k[c, :, cols].astype(F32) * v[c, :, cols].astype(F32)
            prod[lane, halo:, :] = product.astype(BF16).astype(F32)
            out = fse[c, 0:1, cols] * prod[lane, pl.ds(halo, rows), :]
            for j in range(1, taps_se):
                out = out + fse[c, j : j + 1, cols] * prod[lane, pl.ds(halo - j, rows), :]
            conv[c, :, cols] = out
            mixed = q[c, :, cols].astype(F32) * out
            acc[:rows, :] += mixed * mixed

    with jax.named_scope("p_short"):
        each(nblk, short_step)

    def row_copy(which, step):
        return remote(row_out.at[which], row_in.at[which, step - 1],
                      row_send.at[which, step - 1], row_recv.at[which, step - 1],
                      {"tp": lax.rem(tp + step, ntp)})

    def send_rows(which):
        total = jnp.sum(jnp.transpose(acc[...]), axis=0, keepdims=True)
        row_out[which] = jnp.broadcast_to(total, row_out.shape[1:])
        for step in range(1, ntp):
            row_copy(which, step).start()

    def sum_rows(which):
        total = row_out[which]
        for step in range(1, ntp):
            row_copy(which, step).wait_recv()
            total = total + row_in[which, step - 1]
        return total[0:1, :]

    def as_column(line):
        return jnp.transpose(jnp.broadcast_to(line, (LANES, line.shape[1])))[:rows, :]

    send_rows(0)
    with jax.named_scope("p_filt2"):
        several(nblk // 2, nblk, filter_step)
    acc[...] = jnp.zeros_like(acc)
    with jax.named_scope("p_scale"):
        scale[...] = as_column(lax.rsqrt(sum_rows(0) * (1.0 / width) + EPSILON))

    def product_step(c):
        load(5, c).wait()
        for i in range(cpb):
            cols = slice(i * LANES, (i + 1) * LANES)
            mixed = q[c, :, cols].astype(F32) * conv[c, :, cols]
            value = mixed * scale[...] * gain[c, :, cols]
            normed[c, :, cols] = value
            zfull[c, taps:, cols] = (km[c, :, cols].astype(F32) * value).astype(BF16)

    with jax.named_scope("p_prod"):
        each(nblk, product_step)

    single(2).wait()
    single(4).wait()

    def adjoint_step(cs):
        with jax.named_scope("p_whead"):
            for c in cs:
                pl.when(ctx < nctx - 1)(lambda: head_mr(c).wait_recv())

        @pl.when((ctx < nctx - 1) & (cs[-1] == nblk - 1))
        def _():
            each(nblk, lambda c: tail_mr(c).start())

        found = [dot(fg[...], gfull[c]) for c in cs]
        mixes = []
        for c, gs in zip(cs, found):
            zs[c] = gs
            gr, gi = gs[:half], gs[half:]
            hr, hi = hs[c, :half, :], hs[c, half:, :]
            mixes.append(spectrum_of(gr * hr + gi * hi, gi * hr - gr * hi))
        found = [dot(inv[:rows, :], mix) for mix in mixes]
        for c, gp in zip(cs, found):
            for i in range(cpb):
                cols = slice(i * LANES, (i + 1) * LANES)
                back, value = gp[:, cols], normed[c, :, cols]
                grad = back * km[c, :, cols].astype(F32)
                qm[c, :, cols] = (back * value).astype(BF16)
                normed[c, :, cols] = grad
                acc[:rows, :] += grad * value

    with jax.named_scope("p_adj"):
        several(0, nblk, adjoint_step)
    send_rows(1)

    def corr_step(cs):
        found = [dot(fz[:, taps:], zfull[c, taps:, :]) for c in cs]
        mixes = []
        for c, value in zip(cs, found):
            gr, gi = zs[c, :half, :], zs[c, half:, :]
            zr, zi = value[:half], value[half:]
            mixes.append(spectrum_of(gr * zr + gi * zi, gi * zr - gr * zi))
            zs[c] = value
        found = [dot(inv[:taps, :], mix) for mix in mixes]
        for c, part in zip(cs, found):
            for p in range(ppb):
                corr[c * ppb + p] = part[:, p * group : (p + 1) * group]

    with jax.named_scope("p_corr1"):
        several(0, nblk // 2, corr_step)

    with jax.named_scope("p_weight"):
        weight = as_column(sum_rows(1))
        coef[...] = weight * (scale[...] * scale[...]) * (1.0 / width)

    def edge_step(c):
        for i in range(cpb):
            cols = slice(i * LANES, (i + 1) * LANES)
            at = pl.ds(pl.multiple_of(c * blk + i * LANES, LANES), LANES)
            quer = q[c, :halo, cols].astype(F32)
            mixed = quer * conv[c, :halo, cols]
            back = normed[c, :halo, cols] * scale[:halo, :]
            gm = gain[c, :, cols] * back - mixed * coef[:halo, :]
            head_out[:, at] = (gm * quer).astype(BF16)

    each(nblk, edge_step)
    pl.when(ctx > 0)(head_se.start)

    with jax.named_scope("p_corr2"):
        several(nblk // 2, nblk, corr_step)

    mine = ctx // ratio

    def part_of(s, i, other):
        index = 0
        for n, bit in enumerate(bits):
            size = bit // ratio
            own = lax.rem(mine // size, 2)
            if n < s:
                index = index + own * size
            elif n == s:
                index = index + (1 - own if other else own) * size
            else:
                index = index + lax.rem(i // 2 ** (n - s - 1), 2) * size
        return index

    def span(s):
        count = parts >> (s + 1)
        return parts - 2 * count, count

    def halve_copy(s):
        begin, count = span(s)
        bit = bits[s]
        partner = ctx + bit - 2 * bit * lax.rem(ctx // bit, 2)
        where = pl.ds(begin, count)
        return remote(away.at[where], got.at[where], halve_send.at[s], halve_recv.at[s],
                      {"ctx": partner})

    def halve_start(s):
        begin, count = span(s)

        def body(i):
            away[begin + i] = corr[part_of(s, i, True)].astype(BF16)

        each(count, body)
        halve_copy(s).start()

    def halve_end(s):
        begin, count = span(s)
        halve_copy(s).wait_recv()

        def body(i):
            corr[part_of(s, i, False)] += got[begin + i].astype(F32)

        each(count, body)

    halve_start(0)

    with jax.named_scope("p_headse"):
        pl.when(ctx < nctx - 1)(head_se.wait_recv)

    high = next(n for n in (32, 16, rows) if rows % n == 0)
    lanes = runs(cpb)

    def back_lane(c, i, n):
        cols = pl.ds(pl.multiple_of(i * LANES, LANES), LANES)
        lane = c * cpb + i
        at = pl.ds(pl.multiple_of(lane * LANES, LANES), LANES)
        pad_g[n, rows:, :] = head_in[:, at].astype(F32)
        gains = jnp.zeros((8, LANES), F32)
        sums = [jnp.zeros((8, LANES), F32) for _ in range(taps_se)]

        def fold(value):
            return jnp.sum(value.reshape(-1, 8, LANES), axis=0)

        taps_of = [fse[c, j : j + 1, cols] for j in range(taps_se)]
        gain_of = gain[c, :, cols]
        for start in range(rows - high, -1, -high):
            at_rows = slice(start, start + high)
            back = normed[c, at_rows, cols] * scale[at_rows, :]
            quer = q[c, at_rows, cols].astype(F32)
            value = conv[c, at_rows, cols]
            mixed = quer * value
            gm = gain_of * back - mixed * coef[at_rows, :]
            gains = gains + fold(back * mixed)
            q[c, at_rows, cols] = (gm * value).astype(BF16)
            gc = (gm * quer).astype(BF16).astype(F32)
            pad_g[n, at_rows, :] = gc
            gp = taps_of[0] * gc
            for j in range(taps_se):
                if j:
                    gp = gp + taps_of[j] * pad_g[n, pl.ds(start + j, high), :]
                sums[j] = sums[j] + fold(gc * prod[lane, pl.ds(start + halo - j, high), :])
            key = k[c, at_rows, cols].astype(F32)
            k[c, at_rows, cols] = (gp * v[c, at_rows, cols].astype(F32)).astype(BF16)
            v[c, at_rows, cols] = (gp * key).astype(BF16)
        part = lane * LANES // group
        place = pl.ds(pl.multiple_of(lax.rem(lane * LANES, group), LANES), LANES)
        for j, value in enumerate(sums + [gains]):
            small[part, j : j + 1, place] = jnp.sum(value, axis=0, keepdims=True)

    def back_step(p):
        c, i = (p * lanes) // cpb, lax.rem(p * lanes, cpb)
        for n in range(lanes):
            back_lane(c, i + n, n)

    def swap(step):
        there = lax.rem(ctx + step, nctx)
        return remote(small.at[there], small_in.at[step - 1], swap_send.at[step - 1],
                      swap_recv.at[step - 1], {"ctx": there})

    def medium_step(cs):
        with jax.named_scope("p_wtail"):
            for c in cs:
                pl.when(ctx > 0)(lambda: tail_mr(c).wait_recv())
        found = [dot(fz[:, :taps], zfull[c, :taps, :]) for c in cs]
        mixes = []
        for c, value in zip(cs, found):
            zr, zi = zs[c, :half, :] + value[:half], zs[c, half:, :] + value[half:]
            hr, hi = hs[c, :half, :], hs[c, half:, :]
            mixes.append(spectrum_of(zr * hr - zi * hi, zr * hi + zi * hr))
        found = [dot(inv[:rows, :], mix) for mix in mixes]
        for c, value in zip(cs, found):
            up[c] = (up[c].astype(F32) * value).astype(BF16)

    def pass_on(s):
        with jax.named_scope("p_halve"):
            halve_end(s)
            if s + 1 < steps:
                halve_start(s + 1)

    steps = len(bits)
    per = nblk * cpb // lanes
    early = per // 4
    with jax.named_scope("p_back"):
        each(early, back_step)
    pass_on(0)
    with jax.named_scope("p_back"):
        each(per - early, back_step, early)
    if ratio == 1:
        for step in range(1, nctx):
            swap(step).start()
    pass_on(1)
    with jax.named_scope("p_medium"):
        several(0, nblk, medium_step)
    for s in range(2, steps):
        pass_on(s)

    with jax.named_scope("p_swap"):
        total_o[...] = corr[mine] * factor
        if ratio == 1:
            value = small[mine]
            for step in range(1, nctx):
                swap(step).wait_recv()
                value = value + small_in[step - 1]
            small_o[...] = value * factor
        else:
            small_o[...] = small[...]

    with jax.named_scope("p_fin"):
        @pl.when(ctx > 0)
        def _():
            each(nblk, lambda c: head_mr(c).wait_send())
            head_se.wait_send()

        @pl.when(ctx < nctx - 1)
        def _():
            each(nblk, lambda c: tail_mr(c).wait_send())
            tail_se.wait_send()

        for which in range(2):
            for step in range(1, ntp):
                row_copy(which, step).wait_send()
        for s in range(steps):
            halve_copy(s).wait_send()
        if ratio == 1:
            for step in range(1, nctx):
                swap(step).wait_send()


def output_kernel(whole, *refs):
    count = 9 if whole else 5
    q, k, v, qm, up, total, small = refs[:7]
    outs, (sems,) = refs[7 : 7 + count], refs[7 + count :]
    gq_o, gk_o, gv_o, gqm_o, gkm_o = outs[:5]
    nblk, rows, blk = q.shape

    def copy(src, dst, s, c):
        at = pl.ds(pl.multiple_of(c * blk, blk), blk)
        return pltpu.make_async_copy(src.at[c], dst.at[:, at], sems.at[s, c])

    streams = ((q, gq_o), (k, gk_o), (v, gv_o), (qm, gkm_o), (up, gqm_o))

    def begin(c, carry):
        for s in range(5):
            copy(*streams[s], s, c).start()
        return carry

    lax.fori_loop(0, nblk, begin, 0)
    if whole:
        filter_se, filter_mr, skip, gain = outs[5:]
        taps_se = filter_se.shape[0]
        filter_se[...] = small[:taps_se, :]
        filter_mr[...] = total[...]
        skip[...] = total[0:1, :]
        gain[...] = small[taps_se : taps_se + 1, :]
    def end(c, carry):
        for s in range(5):
            copy(*streams[s], s, c).wait()
        return carry

    lax.fori_loop(0, nblk, end, 0)


def split_parts(parts, share):
    count, height, group = parts.shape
    if group == share:
        return parts
    parts = parts.reshape(count, height, group // share, share)
    return parts.transpose(0, 2, 1, 3).reshape(-1, height, share)


def scatter_sum(parts, axis, stop):
    size = lax.axis_size(axis)
    me = lax.axis_index(axis)
    bit = 1
    while bit < stop:
        rest = parts.reshape((parts.shape[0] // 2, 2) + parts.shape[1:])
        mine = lax.rem(me // bit, 2)
        away = lax.dynamic_index_in_dim(rest, 1 - mine, 1, keepdims=False).astype(BF16)
        keep = lax.dynamic_index_in_dim(rest, mine, 1, keepdims=False)
        with jax.named_scope(f"halve_{bit}"):
            got = lax.ppermute(away, axis, [(i, i ^ bit) for i in range(size)])
        parts = keep + got.astype(F32)
        bit *= 2
    return parts[0]


def local(
    query_se, key_se, value_se, query_mr, key_mr, upstream, filter_se, filter_mr, skip_mr, norm_gain
):
    rows, chans = query_se.shape
    taps_se, taps = filter_se.shape[0], filter_mr.shape[0]
    ctx, ntp = lax.axis_size("ctx"), lax.axis_size("tp")
    width = chans * ntp
    tokens = rows * ctx
    share = chans // ctx
    group = up_to(share, LANES)
    halo = up_to(taps_se - 1, 16)
    blk = max(group, min(512, chans))
    nblk = chans // blk
    fz, fg, inv = transforms(rows, taps)
    length = rows + taps
    tall = up_to(rows, LANES)
    nlane = chans // LANES

    def out(shape, kind):
        return jax.ShapeDtypeStruct(shape, kind)

    ins = (query_se, key_se, value_se, query_mr, key_mr, upstream, filter_se, filter_mr,
           skip_mr[None], norm_gain[None], fg, fz, inv)
    V, D = pltpu.VMEM, pltpu.SemaphoreType.DMA
    ratio = group // share
    parts = chans // group
    small_height = taps_se + 1
    small_shape = (small_height, group) if ratio == 1 else (parts, small_height, group)
    stream = V((nblk, rows, blk), BF16)
    outs = [stream] * 5 + [V((taps, group), F32), V(small_shape, F32)]
    lanes = runs(blk // LANES)
    steps = len(halving_bits(ctx, ratio))
    scratch = [
        stream, V((nblk, taps_se, blk), F32), V((nblk, taps, blk), F32), V((nblk, 1, blk), F32),
        V((nblk, 1, blk), F32), V(fg.shape, BF16), V(fz.shape, BF16), V(inv.shape, BF16),
        V((2, halo, chans), BF16), V((halo, chans), BF16), V((halo, chans), BF16),
        V((halo, chans), BF16), V((halo, chans), BF16),
        V((nblk, length, blk), BF16), V((nblk, length, blk), BF16),
        V((nblk, rows, blk), F32), V((nblk, rows, blk), F32),
        V((nblk, length, blk), F32), V((nblk, length, blk), F32),
        V((nlane, halo + rows, LANES), F32), V((lanes, halo + rows, LANES), F32),
        V((parts, taps, group), F32), V((parts, small_height, group), F32),
        V((parts, taps, group), BF16), V((parts, taps, group), BF16),
        V((max(ctx - 1, 1), small_height, group), F32),
        V((tall, LANES), F32), V((rows, LANES), F32), V((rows, LANES), F32),
        V((2, 8, tall), F32), V((2, max(ntp - 1, 1), 8, tall), F32),
        D((7, nblk)), D((3, nblk)), D((5,)), D((2,)), D((2,)),
        D((nblk,)), D((nblk,)), D((nblk,)), D((nblk,)),
        D((2, max(ntp - 1, 1))), D((2, max(ntp - 1, 1))),
        D((steps,)), D((steps,)), D((max(ctx - 1, 1),)), D((max(ctx - 1, 1),)),
    ]
    anywhere = pl.BlockSpec(memory_space=pl.ANY)
    inside = pl.BlockSpec(memory_space=pltpu.VMEM)
    with jax.named_scope("layer"):
        held = pl.pallas_call(
            functools.partial(layer_kernel, width, tokens, ctx, ntp, ratio),
            name="layer",
            in_specs=[anywhere] * len(ins),
            out_specs=[inside] * len(outs),
            out_shape=outs,
            scratch_shapes=scratch,
            compiler_params=pltpu.CompilerParams(
                collective_id=0, has_side_effects=True, vmem_limit_bytes=48 * 2**20
            ),
        )(*ins)

    def out(shape, kind):
        return jax.ShapeDtypeStruct(shape, kind)

    results = [out((rows, chans), BF16)] * 5
    specs = [anywhere] * 5
    if ratio == 1:
        results += [out((n, share), F32) for n in (taps_se, taps, 1, 1)]
        specs += [inside] * 4
    with jax.named_scope("output"):
        found = pl.pallas_call(
            functools.partial(output_kernel, ratio == 1),
            name="output",
            in_specs=[inside] * len(held),
            out_specs=specs,
            out_shape=results,
            scratch_shapes=[D((5, nblk))],
            compiler_params=pltpu.CompilerParams(vmem_limit_bytes=8 * 2**20),
        )(*[pltpu.with_memory_space_constraint(a, pltpu.VMEM) for a in held])
    if ratio == 1:
        return (*found[:7], found[7].reshape(share), found[8].reshape(share))
    total_mr, small = held[5], held[6]
    total_mr = scatter_sum(split_parts(total_mr[None], share), "ctx", ratio)
    small = lax.all_to_all(split_parts(small, share), "ctx", 0, 0, tiled=True)
    total = jnp.sum(small, axis=0) * (1.0 / math.sqrt(tokens))
    return (*found, total[:taps_se], total_mr, total_mr[0], total[taps_se])


def solution(mesh):
    streams = (P("ctx", "tp"),)
    in_specs = streams * 6 + (P(None, "tp"), P(None, "tp"), P("tp"), P("tp"))
    both = ("tp", "ctx")
    out_specs = streams * 5 + (P(None, both), P(None, both), P(both), P(both))
    return jax.shard_map(local, mesh=mesh, in_specs=in_specs, out_specs=out_specs, check_vma=False)
```

time: 89.5 us -> 62.3 us (0.70)
  the two profiles are of different devices: /device:TPU:0 before, /device:TPU:24 now
where the time goes in v1:
time: 62.3 us; the launch traced here: 62.1 us
  Pallas kernels  61.5 us (99%)
  between operations  0.65 us (1%)
    pallas_call x1, Pallas kernels, local(): pl.pallas_call(functools.partial(layer_kernel, width, tokens, ctx, ntp, r...  57 us
    pallas_call x1, Pallas kernels, local(): pl.pallas_call(functools.partial(output_kernel, ratio == 1), name='output...  4.53 us

profile of v1, /device:TPU:24, one launch (start us, length us, event | category | flops | bytes accessed | tf_op | source)
XLA Modules:
  0.0 62.1 jit_solution(12178687224549157580)
XLA Ops:
  0.6 57.0 %layer.1 = (bf16[8,224,512]{2,1,0:T(8,128)(2,1)S(1)}, bf16[8,224,512]{2,1,0:T(8,128)(2,1)S(1)}, bf16[8,224,512]{2,1,0:T(8,128)(2,1)S(1)}, bf16[8,224,512]{2,1,0:...) custom-call(bf16[224,4096]{1,0:T(8,128)(2,1)} %refs_0_.1, ...), custom_call_target="tpu_custom_call" | custom-call | tf_op jit(solution)/shard_map/layer/layer/pallas_call | solution.py:612
  57.6 4.5 %output.1 = (bf16[224,4096]{1,0:T(8,128)(2,1)}, bf16[224,4096]{1,0:T(8,128)(2,1)}, bf16[224,4096]{1,0:T(8,128)(2,1)}, bf16[224,4096]{1,0:T(8,128)(2,1)}, bf16[22...) custom-call(bf16[8,224,512]{2,1,0:T(8,128)(2,1)S(1)} %get-tuple-element., ...), custom_call_target="tpu_custom_call" | custom-call | tf_op jit(solution)/shard_map/output/output/pallas_call | solution.py:633

commit v2 on v1

--- a/solution.py
+++ b/solution.py
@@ -48,7 +48,7 @@
     while bit < size:
         bits.append(bit)
         bit *= 2
-    return bits[:1] + bits[2:] + bits[1:2]
+    return bits[:1] + bits[2:3] + bits[1:2] + bits[3:]
 
 
 def runs(count):
@@ -59,13 +59,13 @@
     (q_h, k_h, v_h, qm_h, km_h, up_h, fse_h, fmr_h, skip_h, gain_h, fg_h, fz_h, inv_h,
      q, k, v, qm, up, total_o, small_o,
      km, fse, fmr, skip, gain, fg, fz, inv, ends, tail_out, tail_in, head_out, head_in,
-     gfull, zfull, conv, normed, hs, zs, prod, pad_g, corr, small, away, got, small_in,
+     gfull, zfull, conv, normed, hs, zs, prod, pad_g, lasts, corr, small, away, got, small_in,
      acc, scale, coef, row_out, row_in,
      in_sem, small_sem, edge_sem, edge_send, edge_recv, head_send, head_recv, tail_send, tail_recv,
      row_send, row_recv, halve_send, halve_recv, swap_send, swap_recv) = refs
     nblk, rows, blk = q.shape
     taps_se, taps = fse.shape[1], fmr.shape[1]
-    halo = tail_in.shape[0]
+    edge, halo = ends.shape[1], prod.shape[1] - rows
     half = fg.shape[0] // 2
     parts, _, group = corr.shape
     ppb = parts // nblk
@@ -105,7 +105,7 @@
         return pltpu.make_async_copy(src.at[:, cols_of(c)], dst.at[c], small_sem.at[s, c])
 
     def single(s):
-        bottom = pl.ds(rows - halo, halo)
+        bottom = pl.ds(rows - edge, edge)
         src, dst = ((k_h.at[bottom, :], ends.at[0]), (v_h.at[bottom, :], ends.at[1]),
                     (fg_h, fg), (fz_h, fz), (inv_h, inv))[s]
         return pltpu.make_async_copy(src, dst, edge_sem.at[s])
@@ -163,7 +163,16 @@
 
     single(0).wait()
     single(1).wait()
-    tail_out[...] = (ends[0].astype(F32) * ends[1].astype(F32)).astype(BF16)
+    ending = (ends[0].astype(F32) * ends[1].astype(F32))[edge - halo :]
+    middle = nblk // 2
+    tail_out[...] = jnp.concatenate(
+        [ending[:, : middle * blk], ending[:, middle * blk :]], 0
+    ).astype(BF16)
+
+    def received(buffer, c, i):
+        at = pl.ds(pl.multiple_of(lax.rem(c, middle) * blk + i * LANES, LANES), LANES)
+        both = buffer[:, at].astype(F32)
+        return jnp.where(c >= middle, both[halo:], both[:halo])
 
     def gate_step(c):
         load(0, c).wait()
@@ -187,15 +196,22 @@
             hs[c, half:, :] = value[half:]
 
     with jax.named_scope("p_filt1"):
-        several(0, nblk // 2, filter_step)
+        several(0, nblk // 4, filter_step)
 
     @pl.when(ctx > 0)
     def _():
         each(nblk, lambda c: head_mr(c).start())
 
     acc[...] = jnp.zeros_like(acc)
-    with jax.named_scope("p_tailse"):
-        pl.when(ctx > 0)(tail_se.wait_recv)
+    prod[:, :halo, :] = jnp.zeros((prod.shape[0], halo, LANES), F32)
+
+    def short_conv(c, cols, lane, height):
+        out = fse[c, 0:1, cols] * prod[lane, pl.ds(halo, height), :]
+        for j in range(1, taps_se):
+            out = out + fse[c, j : j + 1, cols] * prod[lane, pl.ds(halo - j, height), :]
+        conv[c, :height, cols] = out
+        mixed = q[c, :height, cols].astype(F32) * out
+        return mixed * mixed
 
     def short_step(c):
         wide(0, c).wait()
@@ -205,19 +221,23 @@
         for i in range(cpb):
             cols = slice(i * LANES, (i + 1) * LANES)
             lane = c * cpb + i
-            at = pl.ds(pl.multiple_of(lane * LANES, LANES), LANES)
-            prod[lane, :halo, :] = tail_in[:, at].astype(F32)
             product = k[c, :, cols].astype(F32) * v[c, :, cols].astype(F32)
             prod[lane, halo:, :] = product.astype(BF16).astype(F32)
-            out = fse[c, 0:1, cols] * prod[lane, pl.ds(halo, rows), :]
-            for j in range(1, taps_se):
-                out = out + fse[c, j : j + 1, cols] * prod[lane, pl.ds(halo - j, rows), :]
-            conv[c, :, cols] = out
-            mixed = q[c, :, cols].astype(F32) * out
-            acc[:rows, :] += mixed * mixed
+            acc[halo:rows, :] += short_conv(c, cols, lane, rows)[halo:]
+
+    def top_step(c):
+        for i in range(cpb):
+            cols = slice(i * LANES, (i + 1) * LANES)
+            lane = c * cpb + i
+            prod[lane, :halo, :] = received(tail_in, c, i)
+            acc[:halo, :] += short_conv(c, cols, lane, halo)
 
     with jax.named_scope("p_short"):
         each(nblk, short_step)
+    with jax.named_scope("p_tailse"):
+        pl.when(ctx > 0)(tail_se.wait_recv)
+    with jax.named_scope("p_top"):
+        each(nblk, top_step)
 
     def row_copy(which, step):
         return remote(row_out.at[which], row_in.at[which, step - 1],
@@ -242,7 +262,7 @@
 
     send_rows(0)
     with jax.named_scope("p_filt2"):
-        several(nblk // 2, nblk, filter_step)
+        several(nblk // 4, nblk, filter_step)
     acc[...] = jnp.zeros_like(acc)
     with jax.named_scope("p_scale"):
         scale[...] = as_column(lax.rsqrt(sum_rows(0) * (1.0 / width) + EPSILON))
@@ -262,24 +282,35 @@
     single(2).wait()
     single(4).wait()
 
+    def tails(start, stop):
+        pl.when(ctx < nctx - 1)(lambda: each(stop - start, lambda c: tail_mr(c).start(), start))
+
+    ahead = nblk * 3 // 8
+    late = lax.rem(ctx, 4) == 3
+
     def adjoint_step(cs):
         with jax.named_scope("p_whead"):
             for c in cs:
                 pl.when(ctx < nctx - 1)(lambda: head_mr(c).wait_recv())
 
-        @pl.when((ctx < nctx - 1) & (cs[-1] == nblk - 1))
+        @pl.when(cs[-1] == nblk - 1)
         def _():
-            each(nblk, lambda c: tail_mr(c).start())
-
-        found = [dot(fg[...], gfull[c]) for c in cs]
-        mixes = []
-        for c, gs in zip(cs, found):
-            zs[c] = gs
+            tails(0, ahead)
+            pl.when(jnp.logical_not(late))(lambda: tails(ahead, nblk))
+
+        gss = [dot(fg[...], gfull[c]) for c in cs]
+        zss = [dot(fz[:, taps:], zfull[c, taps:, :]) for c in cs]
+        mixes, pairs = [], []
+        for c, gs, value in zip(cs, gss, zss):
             gr, gi = gs[:half], gs[half:]
             hr, hi = hs[c, :half, :], hs[c, half:, :]
             mixes.append(spectrum_of(gr * hr + gi * hi, gi * hr - gr * hi))
+            zr, zi = value[:half], value[half:]
+            pairs.append(spectrum_of(gr * zr + gi * zi, gi * zr - gr * zi))
+            zs[c] = value
         found = [dot(inv[:rows, :], mix) for mix in mixes]
-        for c, gp in zip(cs, found):
+        parts_of = [dot(inv[:taps, :], mix) for mix in pairs]
+        for c, gp, part in zip(cs, found, parts_of):
             for i in range(cpb):
                 cols = slice(i * LANES, (i + 1) * LANES)
                 back, value = gp[:, cols], normed[c, :, cols]
@@ -287,47 +318,12 @@
                 qm[c, :, cols] = (back * value).astype(BF16)
                 normed[c, :, cols] = grad
                 acc[:rows, :] += grad * value
+            for p in range(ppb):
+                corr[c * ppb + p] = part[:, p * group : (p + 1) * group]
 
     with jax.named_scope("p_adj"):
         several(0, nblk, adjoint_step)
     send_rows(1)
-
-    def corr_step(cs):
-        found = [dot(fz[:, taps:], zfull[c, taps:, :]) for c in cs]
-        mixes = []
-        for c, value in zip(cs, found):
-            gr, gi = zs[c, :half, :], zs[c, half:, :]
-            zr, zi = value[:half], value[half:]
-            mixes.append(spectrum_of(gr * zr + gi * zi, gi * zr - gr * zi))
-            zs[c] = value
-        found = [dot(inv[:taps, :], mix) for mix in mixes]
-        for c, part in zip(cs, found):
-            for p in range(ppb):
-                corr[c * ppb + p] = part[:, p * group : (p + 1) * group]
-
-    with jax.named_scope("p_corr1"):
-        several(0, nblk // 2, corr_step)
-
-    with jax.named_scope("p_weight"):
-        weight = as_column(sum_rows(1))
-        coef[...] = weight * (scale[...] * scale[...]) * (1.0 / width)
-
-    def edge_step(c):
-        for i in range(cpb):
-            cols = slice(i * LANES, (i + 1) * LANES)
-            at = pl.ds(pl.multiple_of(c * blk + i * LANES, LANES), LANES)
-            quer = q[c, :halo, cols].astype(F32)
-            mixed = quer * conv[c, :halo, cols]
-            back = normed[c, :halo, cols] * scale[:halo, :]
-            gm = gain[c, :, cols] * back - mixed * coef[:halo, :]
-            head_out[:, at] = (gm * quer).astype(BF16)
-
-    each(nblk, edge_step)
-    pl.when(ctx > 0)(head_se.start)
-
-    with jax.named_scope("p_corr2"):
-        several(nblk // 2, nblk, corr_step)
-
     mine = ctx // ratio
 
     def part_of(s, i, other):
@@ -373,10 +369,37 @@
 
         each(count, body)
 
+    steps = len(bits)
+
+    def pass_on(s):
+        with jax.named_scope("p_halve"):
+            halve_end(s)
+            if s + 1 < steps:
+                halve_start(s + 1)
+
     halve_start(0)
-
-    with jax.named_scope("p_headse"):
-        pl.when(ctx < nctx - 1)(head_se.wait_recv)
+    pass_on(0)
+    pl.when(late)(lambda: tails(ahead, nblk))
+
+    with jax.named_scope("p_weight"):
+        weight = as_column(sum_rows(1))
+        coef[...] = weight * (scale[...] * scale[...]) * (1.0 / width)
+
+    def edge_step(c):
+        for i in range(cpb):
+            cols = slice(i * LANES, (i + 1) * LANES)
+            at = pl.ds(pl.multiple_of(c * blk + i * LANES, LANES), LANES)
+            both = []
+            for part in (c, c + middle):
+                quer = q[part, :halo, cols].astype(F32)
+                mixed = quer * conv[part, :halo, cols]
+                back = normed[part, :halo, cols] * scale[:halo, :]
+                gm = gain[part, :, cols] * back - mixed * coef[:halo, :]
+                both.append(gm * quer)
+            head_out[:, at] = jnp.concatenate(both, 0).astype(BF16)
+
+    each(middle, edge_step)
+    pl.when(ctx > 0)(head_se.start)
 
     high = next(n for n in (32, 16, rows) if rows % n == 0)
     lanes = runs(cpb)
@@ -384,8 +407,7 @@
     def back_lane(c, i, n):
         cols = pl.ds(pl.multiple_of(i * LANES, LANES), LANES)
         lane = c * cpb + i
-        at = pl.ds(pl.multiple_of(lane * LANES, LANES), LANES)
-        pad_g[n, rows:, :] = head_in[:, at].astype(F32)
+        pad_g[n, rows:, :] = jnp.zeros((halo, LANES), F32)
         gains = jnp.zeros((8, LANES), F32)
         sums = [jnp.zeros((8, LANES), F32) for _ in range(taps_se)]
 
@@ -405,6 +427,8 @@
             q[c, at_rows, cols] = (gm * value).astype(BF16)
             gc = (gm * quer).astype(BF16).astype(F32)
             pad_g[n, at_rows, :] = gc
+            if start + high == rows:
+                lasts[lane, :halo, :] = gc[high - halo :, :]
             gp = taps_of[0] * gc
             for j in range(taps_se):
                 if j:
@@ -417,6 +441,22 @@
         place = pl.ds(pl.multiple_of(lax.rem(lane * LANES, group), LANES), LANES)
         for j, value in enumerate(sums + [gains]):
             small[part, j : j + 1, place] = jnp.sum(value, axis=0, keepdims=True)
+
+    def bottom_step(c):
+        for i in range(cpb):
+            cols = slice(i * LANES, (i + 1) * LANES)
+            lane = c * cpb + i
+            at = pl.ds(pl.multiple_of(lane * LANES, LANES), LANES)
+            lasts[lane, halo:, :] = received(head_in, c, i)
+            gp = fse[c, 0:1, cols] * lasts[lane, :halo, :]
+            for j in range(1, taps_se):
+                gp = gp + fse[c, j : j + 1, cols] * lasts[lane, pl.ds(j, halo), :]
+            for kept, other in ((k, ends[1, :, at]), (v, ends[0, :, at])):
+                old = kept[c, rows - edge :, cols].astype(F32)
+                new = gp * other.astype(F32)[edge - halo :]
+                kept[c, rows - edge :, cols] = jnp.concatenate(
+                    [old[: edge - halo], new], 0
+                ).astype(BF16)
 
     def back_step(p):
         c, i = (p * lanes) // cpb, lax.rem(p * lanes, cpb)
@@ -442,24 +482,20 @@
         for c, value in zip(cs, found):
             up[c] = (up[c].astype(F32) * value).astype(BF16)
 
-    def pass_on(s):
-        with jax.named_scope("p_halve"):
-            halve_end(s)
-            if s + 1 < steps:
-                halve_start(s + 1)
-
-    steps = len(bits)
     per = nblk * cpb // lanes
-    early = per // 4
+    early = per // 2
     with jax.named_scope("p_back"):
         each(early, back_step)
-    pass_on(0)
+    pass_on(1)
     with jax.named_scope("p_back"):
         each(per - early, back_step, early)
     if ratio == 1:
         for step in range(1, nctx):
             swap(step).start()
-    pass_on(1)
+    with jax.named_scope("p_headse"):
+        pl.when(ctx < nctx - 1)(head_se.wait_recv)
+    with jax.named_scope("p_bottom"):
+        each(nblk, bottom_step)
     with jax.named_scope("p_medium"):
         several(0, nblk, medium_step)
     for s in range(2, steps):
@@ -523,6 +559,7 @@
         filter_mr[...] = total[...]
         skip[...] = total[0:1, :]
         gain[...] = small[taps_se : taps_se + 1, :]
+
     def end(c, carry):
         for s in range(5):
             copy(*streams[s], s, c).wait()
@@ -565,8 +602,8 @@
     tokens = rows * ctx
     share = chans // ctx
     group = up_to(share, LANES)
-    halo = up_to(taps_se - 1, 16)
-    blk = max(group, min(512, chans))
+    halo, edge = up_to(taps_se - 1, 8), up_to(taps_se - 1, 16)
+    blk = max(group, min(512, chans // 2))
     nblk = chans // blk
     fz, fg, inv = transforms(rows, taps)
     length = rows + taps
@@ -586,16 +623,18 @@
     stream = V((nblk, rows, blk), BF16)
     outs = [stream] * 5 + [V((taps, group), F32), V(small_shape, F32)]
     lanes = runs(blk // LANES)
+    message = (2 * halo, chans // 2)
     steps = len(halving_bits(ctx, ratio))
     scratch = [
         stream, V((nblk, taps_se, blk), F32), V((nblk, taps, blk), F32), V((nblk, 1, blk), F32),
         V((nblk, 1, blk), F32), V(fg.shape, BF16), V(fz.shape, BF16), V(inv.shape, BF16),
-        V((2, halo, chans), BF16), V((halo, chans), BF16), V((halo, chans), BF16),
-        V((halo, chans), BF16), V((halo, chans), BF16),
+        V((2, edge, chans), BF16), V(message, BF16), V(message, BF16), V(message, BF16),
+        V(message, BF16),
         V((nblk, length, blk), BF16), V((nblk, length, blk), BF16),
         V((nblk, rows, blk), F32), V((nblk, rows, blk), F32),
         V((nblk, length, blk), F32), V((nblk, length, blk), F32),
         V((nlane, halo + rows, LANES), F32), V((lanes, halo + rows, LANES), F32),
+        V((nlane, 2 * halo, LANES), F32),
         V((parts, taps, group), F32), V((parts, small_height, group), F32),
         V((parts, taps, group), BF16), V((parts, taps, group), BF16),
         V((max(ctx - 1, 1), small_height, group), F32),

time: 62.3 us -> 52.2 us (0.84)
  the two profiles are of different devices: /device:TPU:24 before, /device:TPU:8 now
where the time goes in v2:
time: 52.2 us; the launch traced here: 52 us
  Pallas kernels  51.4 us (98%)
  between operations  0.65 us (1%)
    pallas_call x1, Pallas kernels, local(): pl.pallas_call(functools.partial(layer_kernel, width, tokens, ctx, ntp, r...  46.8 us
    pallas_call x1, Pallas kernels, local(): pl.pallas_call(functools.partial(output_kernel, ratio == 1), name='output...  4.53 us

profile of v2, /device:TPU:8, one launch (start us, length us, event | category | flops | bytes accessed | tf_op | source)
XLA Modules:
  0.0 52.0 jit_solution(15543355601132666494)
XLA Ops:
  0.6 46.8 %layer.1 = (bf16[8,224,512]{2,1,0:T(8,128)(2,1)S(1)}, bf16[8,224,512]{2,1,0:T(8,128)(2,1)S(1)}, bf16[8,224,512]{2,1,0:T(8,128)(2,1)S(1)}, bf16[8,224,512]{2,1,0:...) custom-call(bf16[224,4096]{1,0:T(8,128)(2,1)} %refs_0_.1, ...), custom_call_target="tpu_custom_call" | custom-call | tf_op jit(solution)/shard_map/layer/layer/pallas_call | solution.py:651
  47.5 4.5 %output.1 = (bf16[224,4096]{1,0:T(8,128)(2,1)}, bf16[224,4096]{1,0:T(8,128)(2,1)}, bf16[224,4096]{1,0:T(8,128)(2,1)}, bf16[224,4096]{1,0:T(8,128)(2,1)}, bf16[22...) custom-call(bf16[8,224,512]{2,1,0:T(8,128)(2,1)S(1)} %get-tuple-element., ...), custom_call_target="tpu_custom_call" | custom-call | tf_op jit(solution)/shard_map/output/output/pallas_call | solution.py:672

commit v3 on v2

--- a/solution.py
+++ b/solution.py
@@ -48,7 +48,7 @@
     while bit < size:
         bits.append(bit)
         bit *= 2
-    return bits[:1] + bits[2:3] + bits[1:2] + bits[3:]
+    return bits[:1] + bits[2:] + bits[1:2]
 
 
 def runs(count):
@@ -64,6 +64,7 @@
      in_sem, small_sem, edge_sem, edge_send, edge_recv, head_send, head_recv, tail_send, tail_recv,
      row_send, row_recv, halve_send, halve_recv, swap_send, swap_recv) = refs
     nblk, rows, blk = q.shape
+    batch = runs(nblk)
     taps_se, taps = fse.shape[1], fmr.shape[1]
     edge, halo = ends.shape[1], prod.shape[1] - rows
     half = fg.shape[0] // 2
@@ -98,11 +99,14 @@
 
     def load(s, c):
         src, dst = streams[s]
-        return pltpu.make_async_copy(src.at[:, cols_of(c)], dst.at[c], in_sem.at[s, c])
+        return pltpu.make_async_copy(src.at[:, cols_of(c)], dst.at[c], in_sem.at[s])
 
     def wide(s, c):
         src, dst = ((fse_h, fse), (skip_h, skip), (gain_h, gain))[s]
-        return pltpu.make_async_copy(src.at[:, cols_of(c)], dst.at[c], small_sem.at[s, c])
+        return pltpu.make_async_copy(src.at[:, cols_of(c)], dst.at[c], small_sem.at[s])
+
+    def settle(ref, sem):
+        pltpu.make_async_copy(ref, ref, sem).wait()
 
     def single(s):
         bottom = pl.ds(rows - edge, edge)
@@ -132,8 +136,8 @@
     single(1).start()
     start_group(0, 1)
     single(3).start()
+    start_group(6)
     each(nblk, start_wide)
-    start_group(6)
     start_group(2, 3, 4)
     single(2).start()
     single(4).start()
@@ -155,11 +159,11 @@
 
     def head_mr(c):
         return remote(gfull.at[c, pl.ds(0, taps), :], gfull.at[c, pl.ds(rows, taps), :],
-                      head_send.at[c], head_recv.at[c], before)
+                      head_send.at[0], head_recv.at[c // batch], before)
 
     def tail_mr(c):
         return remote(zfull.at[c, pl.ds(rows, taps), :], zfull.at[c, pl.ds(0, taps), :],
-                      tail_send.at[c], tail_recv.at[c], after)
+                      tail_send.at[0], tail_recv.at[c // batch], after)
 
     single(0).wait()
     single(1).wait()
@@ -174,9 +178,10 @@
         both = buffer[:, at].astype(F32)
         return jnp.where(c >= middle, both[halo:], both[:halo])
 
+    settle(up, in_sem.at[0])
+    settle(qm, in_sem.at[1])
+
     def gate_step(c):
-        load(0, c).wait()
-        load(1, c).wait()
         gfull[c, :rows, :] = (up[c].astype(F32) * qm[c].astype(F32)).astype(BF16)
 
     with jax.named_scope("p_gate"):
@@ -185,11 +190,10 @@
         pl.semaphore_wait(barrier, nctx + ntp - 2)
     pl.when(ctx < nctx - 1)(tail_se.start)
     single(3).wait()
+    settle(fmr, in_sem.at[6])
+    settle(skip, small_sem.at[1])
 
     def filter_step(cs):
-        for c in cs:
-            load(6, c).wait()
-            wide(1, c).wait()
         found = [dot(fz[:, taps : 2 * taps], fmr[c].astype(BF16)) for c in cs]
         for c, value in zip(cs, found):
             hs[c, :half, :] = value[:half] + skip[c]
@@ -213,11 +217,12 @@
         mixed = q[c, :height, cols].astype(F32) * out
         return mixed * mixed
 
+    settle(fse, small_sem.at[0])
+    settle(gain, small_sem.at[2])
+    for s, ref in ((2, k), (3, v), (4, q)):
+        settle(ref, in_sem.at[s])
+
     def short_step(c):
-        wide(0, c).wait()
-        wide(2, c).wait()
-        for s in range(3):
-            load(2 + s, c).wait()
         for i in range(cpb):
             cols = slice(i * LANES, (i + 1) * LANES)
             lane = c * cpb + i
@@ -267,8 +272,9 @@
     with jax.named_scope("p_scale"):
         scale[...] = as_column(lax.rsqrt(sum_rows(0) * (1.0 / width) + EPSILON))
 
+    settle(km, in_sem.at[5])
+
     def product_step(c):
-        load(5, c).wait()
         for i in range(cpb):
             cols = slice(i * LANES, (i + 1) * LANES)
             mixed = q[c, :, cols].astype(F32) * conv[c, :, cols]
@@ -290,8 +296,8 @@
 
     def adjoint_step(cs):
         with jax.named_scope("p_whead"):
-            for c in cs:
-                pl.when(ctx < nctx - 1)(lambda: head_mr(c).wait_recv())
+            part = gfull.at[pl.ds(cs[0], batch), pl.ds(rows, taps), :]
+            pl.when(ctx < nctx - 1)(lambda: settle(part, head_recv.at[cs[0] // batch]))
 
         @pl.when(cs[-1] == nblk - 1)
         def _():
@@ -465,13 +471,13 @@
 
     def swap(step):
         there = lax.rem(ctx + step, nctx)
-        return remote(small.at[there], small_in.at[step - 1], swap_send.at[step - 1],
-                      swap_recv.at[step - 1], {"ctx": there})
+        return remote(small.at[there], small_in.at[step - 1], swap_send.at[0],
+                      swap_recv.at[0], {"ctx": there})
 
     def medium_step(cs):
         with jax.named_scope("p_wtail"):
-            for c in cs:
-                pl.when(ctx > 0)(lambda: tail_mr(c).wait_recv())
+            part = zfull.at[pl.ds(cs[0], batch), pl.ds(0, taps), :]
+            pl.when(ctx > 0)(lambda: settle(part, tail_recv.at[cs[0] // batch]))
         found = [dot(fz[:, :taps], zfull[c, :taps, :]) for c in cs]
         mixes = []
         for c, value in zip(cs, found):
@@ -483,7 +489,7 @@
             up[c] = (up[c].astype(F32) * value).astype(BF16)
 
     per = nblk * cpb // lanes
-    early = per // 2
+    early = per * 3 // 4
     with jax.named_scope("p_back"):
         each(early, back_step)
     pass_on(1)
@@ -505,8 +511,8 @@
         total_o[...] = corr[mine] * factor
         if ratio == 1:
             value = small[mine]
+            settle(small_in, swap_recv.at[0])
             for step in range(1, nctx):
-                swap(step).wait_recv()
                 value = value + small_in[step - 1]
             small_o[...] = value * factor
         else:
@@ -515,12 +521,12 @@
     with jax.named_scope("p_fin"):
         @pl.when(ctx > 0)
         def _():
-            each(nblk, lambda c: head_mr(c).wait_send())
+            settle(gfull.at[:, pl.ds(0, taps), :], head_send.at[0])
             head_se.wait_send()
 
         @pl.when(ctx < nctx - 1)
         def _():
-            each(nblk, lambda c: tail_mr(c).wait_send())
+            settle(zfull.at[:, pl.ds(rows, taps), :], tail_send.at[0])
             tail_se.wait_send()
 
         for which in range(2):
@@ -529,8 +535,7 @@
         for s in range(steps):
             halve_copy(s).wait_send()
         if ratio == 1:
-            for step in range(1, nctx):
-                swap(step).wait_send()
+            settle(small_in, swap_send.at[0])
 
 
 def output_kernel(whole, *refs):
@@ -542,7 +547,7 @@
 
     def copy(src, dst, s, c):
         at = pl.ds(pl.multiple_of(c * blk, blk), blk)
-        return pltpu.make_async_copy(src.at[c], dst.at[:, at], sems.at[s, c])
+        return pltpu.make_async_copy(src.at[c], dst.at[:, at], sems.at[s])
 
     streams = ((q, gq_o), (k, gk_o), (v, gv_o), (qm, gkm_o), (up, gqm_o))
 
@@ -560,12 +565,8 @@
         skip[...] = total[0:1, :]
         gain[...] = small[taps_se : taps_se + 1, :]
 
-    def end(c, carry):
-        for s in range(5):
-            copy(*streams[s], s, c).wait()
-        return carry
-
-    lax.fori_loop(0, nblk, end, 0)
+    for s, (src, _) in enumerate(streams):
+        pltpu.make_async_copy(src, src, sems.at[s]).wait()
 
 
 def split_parts(parts, share):
@@ -640,10 +641,10 @@
         V((max(ctx - 1, 1), small_height, group), F32),
         V((tall, LANES), F32), V((rows, LANES), F32), V((rows, LANES), F32),
         V((2, 8, tall), F32), V((2, max(ntp - 1, 1), 8, tall), F32),
-        D((7, nblk)), D((3, nblk)), D((5,)), D((2,)), D((2,)),
-        D((nblk,)), D((nblk,)), D((nblk,)), D((nblk,)),
+        D((7,)), D((3,)), D((5,)), D((2,)), D((2,)),
+        D((1,)), D((nblk // runs(nblk),)), D((1,)), D((nblk // runs(nblk),)),
         D((2, max(ntp - 1, 1))), D((2, max(ntp - 1, 1))),
-        D((steps,)), D((steps,)), D((max(ctx - 1, 1),)), D((max(ctx - 1, 1),)),
+        D((steps,)), D((steps,)), D((1,)), D((1,)),
     ]
     anywhere = pl.BlockSpec(memory_space=pl.ANY)
     inside = pl.BlockSpec(memory_space=pltpu.VMEM)
@@ -675,7 +676,7 @@
             in_specs=[inside] * len(held),
             out_specs=specs,
             out_shape=results,
-            scratch_shapes=[D((5, nblk))],
+            scratch_shapes=[D((5,))],
             compiler_params=pltpu.CompilerParams(vmem_limit_bytes=8 * 2**20),
         )(*[pltpu.with_memory_space_constraint(a, pltpu.VMEM) for a in held])
     if ratio == 1:

time: 52.2 us -> 50.1 us (0.960)
  the two profiles are of different devices: /device:TPU:8 before, /device:TPU:0 now
where the time goes in v3:
time: 50.1 us; the launch traced here: 49.8 us
  Pallas kernels  49.2 us (98%)
  between operations  0.65 us (1%)
    pallas_call x1, Pallas kernels, local(): pl.pallas_call(functools.partial(layer_kernel, width, tokens, ctx, ntp, r...  45 us
    pallas_call x1, Pallas kernels, local(): pl.pallas_call(functools.partial(output_kernel, ratio == 1), name='output...  4.21 us

profile of v3, /device:TPU:0, one launch (start us, length us, event | category | flops | bytes accessed | tf_op | source)
XLA Modules:
  0.0 49.8 jit_solution(8621138539067876323)
XLA Ops:
  0.6 45.0 %layer.1 = (bf16[8,224,512]{2,1,0:T(8,128)(2,1)S(1)}, bf16[8,224,512]{2,1,0:T(8,128)(2,1)S(1)}, bf16[8,224,512]{2,1,0:T(8,128)(2,1)S(1)}, bf16[8,224,512]{2,1,0:...) custom-call(bf16[224,4096]{1,0:T(8,128)(2,1)} %refs_0_.1, ...), custom_call_target="tpu_custom_call" | custom-call | tf_op jit(solution)/shard_map/layer/layer/pallas_call | solution.py:652
  45.6 4.2 %output.1 = (bf16[224,4096]{1,0:T(8,128)(2,1)}, bf16[224,4096]{1,0:T(8,128)(2,1)}, bf16[224,4096]{1,0:T(8,128)(2,1)}, bf16[224,4096]{1,0:T(8,128)(2,1)}, bf16[22...) custom-call(bf16[8,224,512]{2,1,0:T(8,128)(2,1)S(1)} %get-tuple-element., ...), custom_call_target="tpu_custom_call" | custom-call | tf_op jit(solution)/shard_map/output/output/pallas_call | solution.py:673
